TPU v7x, 256 devices: a whole 4x4x8 slice. The times are simulated.
256 devices in a mesh: dp: 16 (over z_hi, x), blk: 16 (over y, z_lo, core).
Axes of the slice: x: 4, y: 4, z: 8 (z_hi: 4, z_lo: 2; z = z_hi * 2 + z_lo), core: 2. Of those that a mesh axis runs over, the one named last changes fastest.
Arguments:
- queries: bfloat16 [16, 2048, 2048], P('dp', 'blk'), may hold values from -6 to 6
- keys: bfloat16 [16, 2048, 512], P('dp', 'blk'), may hold values from -6 to 6
- values: bfloat16 [16, 2048, 512], P('dp', 'blk'), may hold values from -6 to 6
- out_grad: bfloat16 [16, 2048, 2048], P('dp', 'blk'), may hold values from -6 to 6
- layer_input: bfloat16 [16, 2048, 4096], P('dp', 'blk'), may hold values from -6 to 6
- lengths: int32 [16, 3], P('dp'), may hold values from 128 to 1792, as said below
Outputs:
- query_grad: bfloat16 [16, 2048, 2048], P('dp', 'blk')
- key_grad: bfloat16 [16, 2048, 512], P('dp', 'blk')
- value_grad: bfloat16 [16, 2048, 512], P('dp', 'blk')
- weight_grad: float32 [4096, 1024], P(('dp', 'blk'))
Inputs may be any that keep to these rules, and one draw needn't show every extreme that they name: `lengths`: each row sums to 2048; the chosen and rejected counts lie between 128 and 384.
All inputs are finite; a program needn't handle non-finite values.
Results may differ from a plain program's by a relative error of at most 0.023.
Values may be sent and summed in bfloat16 or wider, within the bound.
A program may use at most 128 MiB of HBM per device.

v0:
```python
import math
import jax
import jax.numpy as jnp
from jax import lax
from jax.sharding import PartitionSpec as P

HEAD = 128
rope_base = 500000.0
masked_fill = -1e30


def side_by_side(arrays, axis, dim, along):
    widths = [a.shape[along] for a in arrays]
    both = jnp.concatenate(arrays, axis=along)
    whole = lax.all_gather(both, axis, axis=dim, tiled=True)
    return tuple(jnp.split(whole, [sum(widths[:k]) for k in range(1, len(widths))], axis=along))


def in_one_piece(arrays, axis, dim, along):
    widths = [a.shape[along] for a in arrays]
    both = jnp.concatenate(arrays, axis=along)
    whole = lax.psum_scatter(both, axis, scatter_dimension=dim, tiled=True)
    return tuple(jnp.split(whole, [sum(widths[:k]) for k in range(1, len(widths))], axis=along))


def cut_along(array, dim, count):
    before, after = (array.shape[:dim], array.shape[dim + 1 :])
    return jnp.moveaxis(array.reshape(*before, count, -1, *after), dim, 0)


def sum_at_owner(array, axis, dim):
    pieces = cut_along(array, dim, lax.axis_size(axis))
    arrived = lax.all_to_all(pieces, axis, split_axis=0, concat_axis=0, tiled=True)
    return arrived.astype(jnp.float32).sum(axis=0)


def stored_positions(stored_rows, shard_rows, shard_count):
    half_rows = shard_rows // 2
    block_number = stored_rows // half_rows
    holder = block_number // 2
    upper_half = block_number % 2
    position_block = jnp.where(upper_half == 1, 2 * shard_count - 1 - holder, holder)
    return (position_block * half_rows + stored_rows % half_rows).astype(jnp.int32)


def allowed_pairs(query_pos, key_pos, prompt_len, chosen_len):
    causal = key_pos[None, :] <= query_pos[:, None]
    reject_start = prompt_len + chosen_len
    query_rejected = query_pos >= reject_start
    key_chosen = jnp.logical_and(key_pos >= prompt_len, key_pos < reject_start)
    return jnp.logical_and(
        causal, jnp.logical_not(jnp.logical_and(query_rejected[:, None], key_chosen[None, :]))
    )


def block_length(total_rows):
    chosen_size = 1
    for candidate in range(1, min(total_rows, 512) + 1):
        if total_rows % candidate == 0:
            chosen_size = candidate
    return chosen_size


def over_blocks(running, pieces, first_row, block_fn):
    total_rows = pieces[0].shape[0]
    block_rows = block_length(total_rows)

    def one_turn(turn_index, current):
        block_start = turn_index * block_rows
        block_parts = tuple(
            (lax.dynamic_slice_in_dim(member, block_start, block_rows, 0) for member in pieces)
        )
        return block_fn(current, block_parts, first_row + block_start)

    return lax.fori_loop(0, total_rows // block_rows, one_turn, running)


def keep_state(running):
    return running


def body(queries, keys, values, out_grad, layer_input, lengths):
    shard_count = lax.axis_size("blk")
    shard_index = lax.axis_index("blk")
    shard_rows = queries.shape[1]
    kv_heads = keys.shape[2] // HEAD
    group_heads = queries.shape[2] // keys.shape[2]
    seq_len = shard_rows * shard_count
    query_count = group_heads * shard_rows
    scale = 1.0 / math.sqrt(HEAD)
    prompt_len = lengths[0, 0]
    chosen_len = lengths[0, 1]
    own_rows = shard_index * shard_rows + jnp.arange(shard_rows, dtype=jnp.int32)
    own_pos = stored_positions(own_rows, shard_rows, shard_count)
    query_pos = jnp.tile(own_pos, group_heads)
    query_rows = (
        queries[0]
        .reshape(shard_rows, kv_heads, group_heads, HEAD)
        .transpose(1, 2, 0, 3)
        .reshape(kv_heads, query_count, HEAD)
    )
    grad_rows = (
        out_grad[0]
        .reshape(shard_rows, kv_heads, group_heads, HEAD)
        .transpose(1, 2, 0, 3)
        .reshape(kv_heads, query_count, HEAD)
    )

    def block_allowed(first_row, count_rows):
        key_pos = stored_positions(
            first_row + jnp.arange(count_rows, dtype=jnp.int32), shard_rows, shard_count
        )
        return allowed_pairs(query_pos, key_pos, prompt_len, chosen_len)

    def forward_block(running, block_parts, first_row):
        key_block, value_block = block_parts
        count_rows = key_block.shape[0]
        allowed = block_allowed(first_row, count_rows)

        def forward_compute(current):
            run_max, run_sum, run_acc = current
            key_heads = key_block.reshape(count_rows, kv_heads, HEAD)
            value_heads = value_block.reshape(count_rows, kv_heads, HEAD).astype(jnp.float32)
            scores = scale * jnp.einsum(
                "gqe,kge->gqk", query_rows, key_heads, preferred_element_type=jnp.float32
            )
            new_max = jnp.maximum(
                run_max, jnp.max(jnp.where(allowed[None], scores, masked_fill), axis=-1)
            )
            weights = jnp.where(allowed[None], jnp.exp(scores - new_max[..., None]), 0.0)
            factor = jnp.exp(run_max - new_max)
            new_sum = run_sum * factor + jnp.sum(weights, axis=-1)
            new_acc = run_acc * factor[..., None] + jnp.einsum(
                "gqk,kge->gqe", weights, value_heads, precision=lax.Precision.HIGHEST
            )
            return (new_max, new_sum, new_acc)

        return lax.cond(jnp.any(allowed), forward_compute, keep_state, running)

    start_forward = (
        jnp.full((kv_heads, query_count), masked_fill, jnp.float32),
        jnp.zeros((kv_heads, query_count), jnp.float32),
        jnp.zeros((kv_heads, query_count, HEAD), jnp.float32),
    )
    run_max, run_sum, run_acc = over_blocks(
        start_forward, side_by_side((keys[0], values[0]), "blk", 0, 1), jnp.int32(0), forward_block
    )
    attn_out = run_acc / run_sum[..., None]
    log_total = run_max + jnp.log(run_sum)
    delta = jnp.sum(grad_rows.astype(jnp.float32) * attn_out, axis=-1)

    def backward_block(running, block_parts, first_row):
        key_block, value_block = block_parts
        count_rows = key_block.shape[0]
        allowed = block_allowed(first_row, count_rows)

        def backward_compute(current):
            query_acc, key_acc, value_acc = current
            key_heads = key_block.reshape(count_rows, kv_heads, HEAD)
            value_heads = value_block.reshape(count_rows, kv_heads, HEAD)
            scores = scale * jnp.einsum(
                "gqe,kge->gqk", query_rows, key_heads, preferred_element_type=jnp.float32
            )
            probs = jnp.where(allowed[None], jnp.exp(scores - log_total[..., None]), 0.0)
            prob_half = probs.astype(jnp.bfloat16)
            prob_grad = jnp.einsum(
                "gqe,kge->gqk", grad_rows, value_heads, preferred_element_type=jnp.float32
            )
            score_grad = (scale * probs * (prob_grad - delta[..., None])).astype(jnp.bfloat16)
            query_acc = query_acc + jnp.einsum(
                "gqk,kge->gqe", score_grad, key_heads, preferred_element_type=jnp.float32
            )
            key_term = jnp.einsum(
                "gqk,gqe->kge", score_grad, query_rows, preferred_element_type=jnp.float32
            ).reshape(count_rows, kv_heads * HEAD)
            value_term = jnp.einsum(
                "gqk,gqe->kge", prob_half, grad_rows, preferred_element_type=jnp.float32
            ).reshape(count_rows, kv_heads * HEAD)
            key_acc = lax.dynamic_update_slice_in_dim(
                key_acc,
                lax.dynamic_slice_in_dim(key_acc, first_row, count_rows, 0) + key_term,
                first_row,
                0,
            )
            value_acc = lax.dynamic_update_slice_in_dim(
                value_acc,
                lax.dynamic_slice_in_dim(value_acc, first_row, count_rows, 0) + value_term,
                first_row,
                0,
            )
            return (query_acc, key_acc, value_acc)

        return lax.cond(jnp.any(allowed), backward_compute, keep_state, running)

    start_backward = (
        jnp.zeros((kv_heads, query_count, HEAD), jnp.float32),
        jnp.zeros((seq_len, kv_heads * HEAD), jnp.float32),
        jnp.zeros((seq_len, kv_heads * HEAD), jnp.float32),
    )
    query_acc, key_acc, value_acc = over_blocks(
        start_backward,
        side_by_side((keys[0], values[0]), "blk", 0, 1),
        jnp.int32(0),
        backward_block,
    )
    key_sum, value_sum = tuple(
        (
            part.astype(jnp.float32)
            for part in in_one_piece(
                (key_acc.astype(jnp.bfloat16), value_acc.astype(jnp.bfloat16)), "blk", 0, 1
            )
        )
    )
    query_grad = (
        query_acc.reshape(kv_heads, group_heads, shard_rows, HEAD)
        .transpose(2, 0, 1, 3)
        .reshape(shard_rows, kv_heads * group_heads * HEAD)
        .astype(jnp.bfloat16)
    )
    key_out = key_sum.astype(jnp.bfloat16)
    value_out = value_sum.astype(jnp.bfloat16)
    half_dim = HEAD // 2
    frequency = jnp.exp(
        -(2.0 * jnp.arange(half_dim, dtype=jnp.float32) / HEAD) * math.log(rope_base)
    )
    angles = own_pos.astype(jnp.float32)[:, None] * frequency[None, :]
    cosine = jnp.concatenate([jnp.cos(angles), jnp.cos(angles)], axis=-1)[:, None, :]
    sine = jnp.concatenate([jnp.sin(angles), jnp.sin(angles)], axis=-1)[:, None, :]
    grad_heads = key_sum.reshape(shard_rows, kv_heads, HEAD)
    rotated = jnp.concatenate([-grad_heads[..., half_dim:], grad_heads[..., :half_dim]], axis=-1)
    key_pre = (
        (grad_heads * cosine - rotated * sine)
        .reshape(shard_rows, kv_heads * HEAD)
        .astype(jnp.bfloat16)
    )
    grad_cols = jnp.concatenate([key_pre, value_out], axis=1)
    input_rows = layer_input[0]
    features = layer_input.shape[2]
    replica_count = lax.axis_size("dp")
    feature_share = features // (replica_count * shard_count)
    grouped_input = input_rows.reshape(shard_rows, replica_count, shard_count * feature_share)
    sequence_input = lax.all_to_all(grouped_input, "blk", split_axis=2, concat_axis=0, tiled=True)
    sequence_weight = jnp.einsum(
        "tif,tc->ifc",
        sequence_input,
        lax.all_gather(grad_cols, "blk", axis=0, tiled=True),
        preferred_element_type=jnp.float32,
    )
    weight_grad = sum_at_owner(sequence_weight.astype(jnp.bfloat16), "dp", 0).reshape(
        feature_share, grad_cols.shape[1]
    )
    return (query_grad[None], key_out[None], value_out[None], weight_grad)


def solution(mesh):
    placed = (
        P("dp", "blk", None),
        P("dp", "blk", None),
        P("dp", "blk", None),
        P("dp", "blk", None),
        P("dp", "blk", None),
        P("dp", None),
    )
    return jax.shard_map(
        body,
        mesh=mesh,
        in_specs=placed,
        out_specs=(
            P("dp", "blk", None),
            P("dp", "blk", None),
            P("dp", "blk", None),
            P(("dp", "blk"), None),
        ),
        check_vma=False,
    )
```

profile of v0, /device:TPU:1, one launch (start us, length us, event | category | flops | bytes accessed | tf_op | source)
XLA Modules:
  0.0 340.4 jit_solution(7980959696925305144)
XLA Ops:
  7.2 1.1 copy.84
  10.1 1.4 reshape_squeeze.9
  16.5 46.8 %all-gather.3.cloned.1.call-done = bf16[2048,1024]{0,1:T(8,128)(2,1)} async-done(((bf16[128,1024]{0,1:T(8,128)(2,1)}), bf16[2048,1024]{0,1:T(8,128)(2,1)}) %all-gather.3.cloned.1.call-update) | async-done | bytes 4194320 | tf_op jit(solution)/shard_map/all_gather | solution.py:15
  63.3 4.8 %fusion.55 = (bf16[2048,512]{0,1:T(8,128)(2,1)}, bf16[2048,512]{0,1:T(8,128)(2,1)}) fusion(bf16[2048,1024]{0,1:T(8,128)(2,1)} %all-gather.3.cloned.1.call-done), kind=kLoop, calls=%fused_computation.129 | loop fusion | bytes 8388608 | tf_op jit(solution)/shard_map/split | solution.py:16
  68.1 39.9 %while.44 = (s32[]{:T(128)}, f32[4,512]{1,0:T(4,128)S(1)}, f32[4,512]{1,0:T(4,128)S(1)}, f32[4,512,128]{2,1,0:T(8,128)S(1)}, s32[]{:T(128)}, /*index=5*/s32[]{:T...) while((s32[]{:T(128)}, f32[4,512]{1,0:T(4,128)S(1)}, ...), condition=%wide.region_6.7_spmd.clone.clone, body=%wide.region_0.6_spmd.clone.clone.sunk | while | flops 1891420160 | bytes 19541308 | solution.py:75
  70.4 7.7 %conditional.8 = ((f32[4,512]{1,0:T(4,128)S(1)}, f32[4,512]{1,0:T(4,128)S(1)}, f32[4,512,128]{2,1,0:T(8,128)S(1)})) conditional(s32[]{:T(128)} %convert_element_type.118, (f32[4,512]{1,0:T(4,128)S(1)}, f32[4,512]{1,0:T(4,128)S(1)}, f32[4,512,128]{2,1,0:T(8,128)S(1)}) %tuple.160, (pred[512,512]{0,1:T(8,128)(4,1)S(1)}, s32[]{:T(128)}, ...), branch_computations={%region_2.2_spmd, %region_3.5_spmd} | conditional | flops 1890062336 | bytes 19267654 | solution.py:138
  70.4 1.3 constant_dynamic-slice_fusion
  73.6 4.4 %fusion.18 = f32[4,512,128]{2,1,0:T(8,128)S(1)} fusion(bf16[512,4,128]{0,2,1:T(8,128)(2,1)S(1)} %bitcast.111, f32[4,512,512]{2,1,0:T(8,128)S(1)} %get-tuple-element.1214, f32[4,512]{1,0:T(4,128)S(1)} %max.5, pred[512,512]{0,1:T(8,128)(4,1)S(1)} %get-tuple-element.924, f32[4,512,128]{2,1,0:T(8,128)S(1)} %get-tuple-element.929, ...), kind=kOutput, calls=%fused_computation.15 | convolution fusion | flops 1614282752 | bytes 7094272 | tf_op jit(solution)/shard_map/while/body/eval_jaxpr/cond/branch_1_fun/gqk,kge->gqe/dot_general | solution.py:133
  80.3 7.7 %conditional.8 = ((f32[4,512]{1,0:T(4,128)S(1)}, f32[4,512]{1,0:T(4,128)S(1)}, f32[4,512,128]{2,1,0:T(8,128)S(1)})) conditional(s32[]{:T(128)} %convert_element_type.118, (f32[4,512]{1,0:T(4,128)S(1)}, f32[4,512]{1,0:T(4,128)S(1)}, f32[4,512,128]{2,1,0:T(8,128)S(1)}) %tuple.160, (pred[512,512]{0,1:T(8,128)(4,1)S(1)}, s32[]{:T(128)}, ...), branch_computations={%region_2.2_spmd, %region_3.5_spmd} | conditional | flops 1890062336 | bytes 19267654 | solution.py:138
  80.4 1.3 constant_dynamic-slice_fusion
  83.6 4.4 %fusion.18 = f32[4,512,128]{2,1,0:T(8,128)S(1)} fusion(bf16[512,4,128]{0,2,1:T(8,128)(2,1)S(1)} %bitcast.111, f32[4,512,512]{2,1,0:T(8,128)S(1)} %get-tuple-element.1214, f32[4,512]{1,0:T(4,128)S(1)} %max.5, pred[512,512]{0,1:T(8,128)(4,1)S(1)} %get-tuple-element.924, f32[4,512,128]{2,1,0:T(8,128)S(1)} %get-tuple-element.929, ...), kind=kOutput, calls=%fused_computation.15 | convolution fusion | flops 1614282752 | bytes 7094272 | tf_op jit(solution)/shard_map/while/body/eval_jaxpr/cond/branch_1_fun/gqk,kge->gqe/dot_general | solution.py:133
  90.3 7.7 %conditional.8 = ((f32[4,512]{1,0:T(4,128)S(1)}, f32[4,512]{1,0:T(4,128)S(1)}, f32[4,512,128]{2,1,0:T(8,128)S(1)})) conditional(s32[]{:T(128)} %convert_element_type.118, (f32[4,512]{1,0:T(4,128)S(1)}, f32[4,512]{1,0:T(4,128)S(1)}, f32[4,512,128]{2,1,0:T(8,128)S(1)}) %tuple.160, (pred[512,512]{0,1:T(8,128)(4,1)S(1)}, s32[]{:T(128)}, ...), branch_computations={%region_2.2_spmd, %region_3.5_spmd} | conditional | flops 1890062336 | bytes 19267654 | solution.py:138
  90.3 1.3 constant_dynamic-slice_fusion
  93.6 4.4 %fusion.18 = f32[4,512,128]{2,1,0:T(8,128)S(1)} fusion(bf16[512,4,128]{0,2,1:T(8,128)(2,1)S(1)} %bitcast.111, f32[4,512,512]{2,1,0:T(8,128)S(1)} %get-tuple-element.1214, f32[4,512]{1,0:T(4,128)S(1)} %max.5, pred[512,512]{0,1:T(8,128)(4,1)S(1)} %get-tuple-element.924, f32[4,512,128]{2,1,0:T(8,128)S(1)} %get-tuple-element.929, ...), kind=kOutput, calls=%fused_computation.15 | convolution fusion | flops 1614282752 | bytes 7094272 | tf_op jit(solution)/shard_map/while/body/eval_jaxpr/cond/branch_1_fun/gqk,kge->gqe/dot_general | solution.py:133
  100.3 7.7 %conditional.8 = ((f32[4,512]{1,0:T(4,128)S(1)}, f32[4,512]{1,0:T(4,128)S(1)}, f32[4,512,128]{2,1,0:T(8,128)S(1)})) conditional(s32[]{:T(128)} %convert_element_type.118, (f32[4,512]{1,0:T(4,128)S(1)}, f32[4,512]{1,0:T(4,128)S(1)}, f32[4,512,128]{2,1,0:T(8,128)S(1)}) %tuple.160, (pred[512,512]{0,1:T(8,128)(4,1)S(1)}, s32[]{:T(128)}, ...), branch_computations={%region_2.2_spmd, %region_3.5_spmd} | conditional | flops 1890062336 | bytes 19267654 | solution.py:138
  100.3 1.3 constant_dynamic-slice_fusion
  103.6 4.4 %fusion.18 = f32[4,512,128]{2,1,0:T(8,128)S(1)} fusion(bf16[512,4,128]{0,2,1:T(8,128)(2,1)S(1)} %bitcast.111, f32[4,512,512]{2,1,0:T(8,128)S(1)} %get-tuple-element.1214, f32[4,512]{1,0:T(4,128)S(1)} %max.5, pred[512,512]{0,1:T(8,128)(4,1)S(1)} %get-tuple-element.924, f32[4,512,128]{2,1,0:T(8,128)S(1)} %get-tuple-element.929, ...), kind=kOutput, calls=%fused_computation.15 | convolution fusion | flops 1614282752 | bytes 7094272 | tf_op jit(solution)/shard_map/while/body/eval_jaxpr/cond/branch_1_fun/gqk,kge->gqe/dot_general | solution.py:133
  108.4 1.2 multiply_reduce_fusion
  109.7 2.5 broadcast.1267
  112.2 2.5 broadcast.1267.clone
  114.7 53.3 %while.45 = (s32[]{:T(128)}, f32[4,512,128]{2,1,0:T(8,128)S(1)}, f32[2048,512]{0,1:T(8,128)}, f32[2048,512]{0,1:T(8,128)}, s32[]{:T(128)}, /*index=5*/s32[]{:T(1...) while((s32[]{:T(128)}, f32[4,512,128]{2,1,0:T(8,128)S(1)}, ...), condition=%wide.region_12.13_spmd.clone.clone, body=%wide.region_8.12_spmd.clone.clone.sunk | while | flops 1355855872 | bytes 35949944 | solution.py:75
  115.4 1.0 fusion.79
  117.0 11.0 %conditional.9 = ((f32[4,512,128]{2,1,0:T(8,128)S(1)}, f32[2048,512]{0,1:T(8,128)}, f32[2048,512]{0,1:T(8,128)})) conditional(s32[]{:T(128)} %convert_element_type.119, (f32[4,512,128]{2,1,0:T(8,128)S(1)}, f32[2048,512]{0,1:T(8,128)}, f32[2048,512]{0,1:T(8,128)}) %tuple.165, (pred[512,512]{0,1:T(8,128)(4,1)S(1)}, s32[]{:T(128)}, ...), branch_computations={%region_10.10_spmd, %region_11.11_spmd} | conditional | flops 1354498048 | bytes 35676240 | solution.py:193
  117.1 1.1 constant_dynamic-slice_fusion.3
  118.9 1.1 constant_dynamic-slice_fusion.2
  120.0 1.7 fusion.23
  121.7 1.2 convolution_add_fusion
  123.7 1.0 fusion.25
  124.7 3.3 constant_dynamic-update-slice_fusion
  128.7 1.0 fusion.79
  130.4 11.0 %conditional.9 = ((f32[4,512,128]{2,1,0:T(8,128)S(1)}, f32[2048,512]{0,1:T(8,128)}, f32[2048,512]{0,1:T(8,128)})) conditional(s32[]{:T(128)} %convert_element_type.119, (f32[4,512,128]{2,1,0:T(8,128)S(1)}, f32[2048,512]{0,1:T(8,128)}, f32[2048,512]{0,1:T(8,128)}) %tuple.165, (pred[512,512]{0,1:T(8,128)(4,1)S(1)}, s32[]{:T(128)}, ...), branch_computations={%region_10.10_spmd, %region_11.11_spmd} | conditional | flops 1354498048 | bytes 35676240 | solution.py:193
  130.4 1.1 constant_dynamic-slice_fusion.3
  132.2 1.1 constant_dynamic-slice_fusion.2
  133.3 1.7 fusion.23
  135.0 1.2 convolution_add_fusion
  137.0 1.0 fusion.25
  138.1 3.3 constant_dynamic-update-slice_fusion
  142.1 1.0 fusion.79
  143.7 10.9 %conditional.9 = ((f32[4,512,128]{2,1,0:T(8,128)S(1)}, f32[2048,512]{0,1:T(8,128)}, f32[2048,512]{0,1:T(8,128)})) conditional(s32[]{:T(128)} %convert_element_type.119, (f32[4,512,128]{2,1,0:T(8,128)S(1)}, f32[2048,512]{0,1:T(8,128)}, f32[2048,512]{0,1:T(8,128)}) %tuple.165, (pred[512,512]{0,1:T(8,128)(4,1)S(1)}, s32[]{:T(128)}, ...), branch_computations={%region_10.10_spmd, %region_11.11_spmd} | conditional | flops 1354498048 | bytes 35676240 | solution.py:193
  143.8 1.1 constant_dynamic-slice_fusion.3
  145.6 1.1 constant_dynamic-slice_fusion.2
  146.7 1.7 fusion.23
  148.4 1.2 convolution_add_fusion
  150.4 1.0 fusion.25
  151.4 3.2 constant_dynamic-update-slice_fusion
  157.0 10.9 %conditional.9 = ((f32[4,512,128]{2,1,0:T(8,128)S(1)}, f32[2048,512]{0,1:T(8,128)}, f32[2048,512]{0,1:T(8,128)})) conditional(s32[]{:T(128)} %convert_element_type.119, (f32[4,512,128]{2,1,0:T(8,128)S(1)}, f32[2048,512]{0,1:T(8,128)}, f32[2048,512]{0,1:T(8,128)}) %tuple.165, (pred[512,512]{0,1:T(8,128)(4,1)S(1)}, s32[]{:T(128)}, ...), branch_computations={%region_10.10_spmd, %region_11.11_spmd} | conditional | flops 1354498048 | bytes 35676240 | solution.py:193
  157.1 1.1 constant_dynamic-slice_fusion.3
  158.9 1.1 constant_dynamic-slice_fusion.2
  160.0 1.7 fusion.23
  161.7 1.2 convolution_add_fusion
  163.7 1.0 fusion.25
  164.7 3.3 constant_dynamic-update-slice_fusion
  168.0 4.6 %copy.91 = bf16[2048,512]{1,0:T(8,128)(2,1)} copy(f32[2048,512]{0,1:T(8,128)} %get-tuple-element.990) | data formatting | bytes 6291456 | tf_op jit(solution)/shard_map/while | solution.py:75
  172.6 4.6 %copy.90 = bf16[2048,512]{1,0:T(8,128)(2,1)} copy(f32[2048,512]{0,1:T(8,128)} %get-tuple-element.989) | data formatting | bytes 6291456 | tf_op jit(solution)/shard_map/while | solution.py:75
  177.2 4.7 %pad_maximum_fusion = bf16[2048,1024]{1,0:T(8,128)(2,1)} fusion(bf16[2048,512]{1,0:T(8,128)(2,1)} %copy.91, bf16[2048,512]{1,0:T(8,128)(2,1)} %copy.90), kind=kLoop, calls=%fused_computation.90 | loop fusion | flops 8388608 | bytes 8388608 | tf_op jit(solution)/shard_map/concatenate | solution.py:21
  182.5 69.4 %reduce-scatter.2.cloned.1.call-done = bf16[128,1024]{1,0:T(8,128)(2,1)} async-done(((bf16[2048,1024]{1,0:T(8,128)(2,1)}), bf16[128,1024]{1,0:T(8,128)(2,1)}) %reduce-scatter.2.cloned.1.call-update) | async-done | bytes 262160 | tf_op jit(solution)/shard_map/reduce_scatter | solution.py:22
  251.9 1.7 slice_convert_fusion
  255.9 1.6 copy.92
  258.2 26.5 %all_to_all.23 = bf16[128,16,256]{0,1,2:T(8,128)(2,1)S(1)} all-to-all(bf16[128,16,256]{0,1,2:T(8,128)(2,1)S(1)} %copy.93), channel_id=1, replica_groups=mesh['dp'=16,'blk'=16] {'blk'}, dimensions={2} | all-to-all | bytes 2097152 | tf_op jit(solution)/shard_map/all_to_all | solution.py:242
  285.4 18.4 %all-gather.5.cloned.1.call-done = bf16[2048,1024]{1,0:T(8,128)(2,1)} async-done(((bf16[128,1024]{1,0:T(8,128)(2,1)}), bf16[2048,1024]{1,0:T(8,128)(2,1)}) %all-gather.5.cloned.1.call-update) | async-done | bytes 4194320 | tf_op jit(solution)/shard_map/all_gather | solution.py:246
  303.8 3.4 %fusion.47 = f32[1024,256]{0,1:S(1)} fusion(bf16[2048,1024]{1,0:T(8,128)(2,1)} %all-gather.5.cloned.1.call-done, bf16[32,8,16,128]{3,2,1,0:T(8,128)(2,1)S(1)} %bitcast.122), kind=kOutput, calls=%fused_computation.91 | convolution fusion | flops 1073741824 | bytes 6291456
  308.1 8.5 %all-to-all-start.1 = ((bf16[16,1,16,1024]{3,2,1,0:T(8,128)(2,1)}), bf16[16,1,16,1024]{3,2,1,0:T(8,128)(2,1)S(1)}, u32[]{:S(2)}, u32[]{:S(2)}) async-start(bf16[16,1,16,1024]{3,2,1,0:T(8,128)(2,1)} %convert_bitcast_fusion), calls=%async_computation.2 | async-start | bytes 1048576 | tf_op jit(solution)/shard_map/all_to_all | solution.py:33
  317.2 1.2 convert_element_type.92
  318.4 14.8 %all-to-all-done.1 = bf16[16,1,16,1024]{3,2,1,0:T(8,128)(2,1)S(1)} async-done(((bf16[16,1,16,1024]{3,2,1,0:T(8,128)(2,1)}), bf16[16,1,16,1024]{3,2,1,0:T(8,128)(2,1)S(1)}, u32[]{:S(2)}, u32[]{:S(2)}) %all-to-all-start.1) | async-done | bytes 524320 | tf_op jit(solution)/shard_map/all_to_all | solution.py:33
  (101 shorter events, 36.5 us)
Async XLA Ops:
  7.2 5.5 %copy-start.1 = (bf16[1,128,2048]{2,1,0:T(8,128)(2,1)S(1)}, bf16[1,128,2048]{2,1,0:T(8,128)(2,1)}, u32[]{:S(2)}) copy-start(bf16[1,128,2048]{2,1,0:T(8,128)(2,1)} %param.17) | copy-start | bytes 1572868
  7.2 56.1 %all-gather.3.cloned.1.call-start = ((), (), s32[]{:S(2)}) async-start(), calls=%async_computation.3 | async-start | bytes 4456448 | tf_op jit(solution)/shard_map/all_gather | solution.py:15
  8.3 6.3 %copy-start.2 = (s32[1,3]{1,0:T(1,128)S(1)}, s32[1,3]{1,0:T(1,128)}, u32[]{:S(2)}) copy-start(s32[1,3]{1,0:T(1,128)} %param.19) | copy-start | bytes 40
  10.1 241.8 %reduce-scatter.2.cloned.1.call-start = ((), (), s32[]{:S(2)}) async-start(), calls=%async_computation.4 | async-start | bytes 4456448 | tf_op jit(solution)/shard_map/reduce_scatter | solution.py:22
  109.7 5.0 %copy-start = (bf16[4,512,128]{1,2,0:T(8,128)(2,1)S(1)}, bf16[4,512,128]{1,2,0:T(8,128)(2,1)}, u32[]{:S(2)}) copy-start(bf16[4,512,128]{1,2,0:T(8,128)(2,1)} %reshape.344) | copy-start | bytes 1572868
  182.0 121.8 %all-gather.5.cloned.1.call-start = ((), (), s32[]{:S(2)}) async-start(), calls=%async_computation.5 | async-start | bytes 4456448 | tf_op jit(solution)/shard_map/all_gather | solution.py:246
  308.1 25.1 %all-to-all-start.1 = ((bf16[16,1,16,1024]{3,2,1,0:T(8,128)(2,1)}), bf16[16,1,16,1024]{3,2,1,0:T(8,128)(2,1)S(1)}, u32[]{:S(2)}, u32[]{:S(2)}) async-start(bf16[16,1,16,1024]{3,2,1,0:T(8,128)(2,1)} %convert_bitcast_fusion), calls=%async_computation.2 | async-start | bytes 1048576 | tf_op jit(solution)/shard_map/all_to_all | solution.py:33
Sparse Core Ops, SparseCore 0:
  10.2 53.0 all-gather.2
  182.1 69.7 reduce-scatter.1
  256.0 47.7 all-gather.4
where the time goes:
time: 342 us; the launch traced here: 340 us
  waiting for transfers between devices  149 us (44%)
  matrix products  47 us (14%)
  local copies, waits for them, and re-layouts  45 us (13%)
  other arithmetic  42.9 us (13%)
  blocking collectives  26.5 us (8%)
  between operations  15.3 us (4%)
  starting transfers between devices  8.67 us (3%)
  loops' own time  5.55 us (2%)
    reduce_scatter x1, waiting for transfers between devices, in_one_piece(): whole = lax.psum_scatter(both, axis, scatter_dimension=dim, tiled=True)  69.4 us
    all_gather x1, waiting for transfers between devices, side_by_side(): whole = lax.all_gather(both, axis, axis=dim, tiled=True)  46.8 us
    all_to_all x1, blocking collectives, body(): lax.all_to_all(grouped_input, 'blk', split_axis=2, concat_axis=0, tiled=T...  26.5 us
    all_gather x1, waiting for transfers between devices, body(): lax.all_gather(grad_cols, 'blk', axis=0, tiled=True)  18.4 us
    dot_general x4, matrix products, forward_compute(): jnp.einsum('gqk,kge->gqe', weights, value_heads, precision=lax.Precision....  17.7 us
    all_to_all x1, waiting for transfers between devices, sum_at_owner(): lax.all_to_all(pieces, axis, split_axis=0, concat_axis=0, tiled=True)  14.8 us
    dynamic_slice x12, local copies, waits for them, and re-layouts, one_turn(): lax.dynamic_slice_in_dim(member, block_start, block_rows, 0)  13.8 us
    dynamic_update_slice x4, other arithmetic, backward_compute(): lax.dynamic_update_slice_in_dim(key_acc, lax.dynamic_slice_in_dim(key_acc...  13 us
  transfers between devices with their start and end apart: 4, of which 4 were waited for; matrix products, arithmetic and copies ran while one was open for 3% of the time, Pallas kernels for 0%

commit v1 on v0

--- a/solution.py
+++ b/solution.py
@@ -7,6 +7,15 @@
 HEAD = 128
 rope_base = 500000.0
 masked_fill = -1e30
+recover_paths = lambda local, axis_id: jnp.concatenate(
+    jax.lax.all_to_all(
+        jnp.stack(jax.lax.psum(1, axis_name=axis_id) * [local]),
+        axis_name=axis_id,
+        split_axis=0,
+        concat_axis=0,
+    ),
+    0,
+)
 
 
 def side_by_side(arrays, axis, dim, along):
@@ -243,7 +252,7 @@
     sequence_weight = jnp.einsum(
         "tif,tc->ifc",
         sequence_input,
-        lax.all_gather(grad_cols, "blk", axis=0, tiled=True),
+        recover_paths(grad_cols, "blk"),
         preferred_element_type=jnp.float32,
     )
     weight_grad = sum_at_owner(sequence_weight.astype(jnp.bfloat16), "dp", 0).reshape(

time: 342 us -> 365 us (1.067)
  blocking collectives: 26.5 us -> 0 us
  waiting for transfers between devices: 149 us -> 175 us
  local copies, waits for them, and re-layouts: 45 us -> 55.8 us
  starting transfers between devices: 8.67 us -> 18.9 us
    all_to_all x0 -> x2, waiting for transfers between devices: none -> 48.3 us  [the longest x1 48.3 us: jax.lax.all_to_all(jnp.stack(jax.lax.psum(1, axis_name=axis_id) * [local]...]
    all_to_all x1 -> x0, blocking collectives: 26.5 us -> none  [body(): lax.all_to_all(grouped_input, 'blk', split_axis=2, concat_axis=0, tiled=T...]
    all_gather x1 -> x0, waiting for transfers between devices: 18.4 us -> none  [body(): lax.all_gather(grad_cols, 'blk', axis=0, tiled=True)]
    all_to_all x0 -> x2, starting transfers between devices: none -> 11 us  [the longest x1 7.24 us: jax.lax.all_to_all(jnp.stack(jax.lax.psum(1, axis_name=axis_id) * [local]...]
    dot_general x0 -> x1, matrix products: none -> 4.54 us  [body(): jnp.einsum('tif,tc->ifc', sequence_input, recover_paths(grad_cols, 'blk')...]
    cond x4 -> x20, local copies, waits for them, and re-layouts: 0.01 us -> 3.92 us
    another operation x4 -> x5, local copies, waits for them, and re-layouts: 5.09 us -> 8.6 us
  transfers between devices with their start and end apart: 4 -> 5, of which waited for: 4 -> 4; matrix products, arithmetic and copies ran while one was open for 3% -> 4% of each run, Pallas kernels for 0% -> 0%
where the time goes in v1:
time: 365 us; the launch traced here: 360 us
  waiting for transfers between devices  175 us (48%)
  local copies, waits for them, and re-layouts  55.8 us (15%)
  matrix products  48.1 us (13%)
  other arithmetic  41.4 us (11%)
  starting transfers between devices  18.9 us (5%)
  between operations  15.6 us (4%)
  loops' own time  5.28 us (1%)
    reduce_scatter x1, waiting for transfers between devices, in_one_piece(): whole = lax.psum_scatter(both, axis, scatter_dimension=dim, tiled=True)  68.6 us
    all_to_all x1, waiting for transfers between devices, jax.lax.all_to_all(jnp.stack(jax.lax.psum(1, axis_name=axis_id) * [local]...  48.3 us
    all_gather x1, waiting for transfers between devices, side_by_side(): whole = lax.all_gather(both, axis, axis=dim, tiled=True)  46.8 us
    dot_general x4, matrix products, forward_compute(): jnp.einsum('gqk,kge->gqe', weights, value_heads, precision=lax.Precision....  17.7 us
    dynamic_slice x12, local copies, waits for them, and re-layouts, one_turn(): lax.dynamic_slice_in_dim(member, block_start, block_rows, 0)  13.2 us
    dynamic_update_slice x4, other arithmetic, backward_compute(): lax.dynamic_update_slice_in_dim(key_acc, lax.dynamic_slice_in_dim(key_acc...  13 us
    while x3, local copies, waits for them, and re-layouts, over_blocks(): return lax.fori_loop(0, total_rows // block_rows, one_turn, running)  12.5 us
    all_to_all x1, waiting for transfers between devices, sum_at_owner(): lax.all_to_all(pieces, axis, split_axis=0, concat_axis=0, tiled=True)  11.8 us
  transfers between devices with their start and end apart: 5, of which 4 were waited for; matrix products, arithmetic and copies ran while one was open for 4% of the time, Pallas kernels for 0%

profile of v1, /device:TPU:1, one launch (start us, length us, event | category | flops | bytes accessed | tf_op | source)
XLA Modules:
  0.0 360.4 jit_solution(15649504833109046702)
XLA Ops:
  7.2 1.1 copy.83
  10.2 1.4 reshape_squeeze.9
  16.5 46.8 %all-gather.2.cloned.1.call-done = bf16[2048,1024]{0,1:T(8,128)(2,1)} async-done(((bf16[128,1024]{0,1:T(8,128)(2,1)}), bf16[2048,1024]{0,1:T(8,128)(2,1)}) %all-gather.2.cloned.1.call-update) | async-done | bytes 4194320 | tf_op jit(solution)/shard_map/all_gather | solution.py:24
  63.3 4.1 %fusion.63 = (bf16[2048,512]{0,1:T(8,128)(2,1)S(1)}, bf16[2048,512]{0,1:T(8,128)(2,1)}) fusion(bf16[2048,1024]{0,1:T(8,128)(2,1)} %all-gather.2.cloned.1.call-done), kind=kLoop, calls=%fused_computation.130 | loop fusion | bytes 8388608 | tf_op jit(solution)/shard_map/split | solution.py:25
  67.3 1.0 broadcast.1268.clone
  68.4 43.1 %while.44 = (s32[]{:T(128)}, f32[4,512]{1,0:T(4,128)S(1)}, f32[4,512]{1,0:T(4,128)S(1)}, f32[4,512,128]{2,1,0:T(8,128)}, s32[]{:T(128)}, /*index=5*/s32[]{:T(128...) while((s32[]{:T(128)}, f32[4,512]{1,0:T(4,128)S(1)}, ...), condition=%wide.region_6.7_spmd.clone.clone, body=%wide.region_0.6_spmd.clone.clone.sunk | while | flops 1891420160 | bytes 27929972 | solution.py:84
  70.6 8.6 %conditional.8 = ((f32[4,512]{1,0:T(4,128)S(1)}, f32[4,512]{1,0:T(4,128)S(1)}, f32[4,512,128]{2,1,0:T(8,128)})) conditional(s32[]{:T(128)} %convert_element_type.120, (f32[4,512]{1,0:T(4,128)S(1)}, f32[4,512]{1,0:T(4,128)S(1)}, f32[4,512,128]{2,1,0:T(8,128)}) %tuple.160, (pred[512,512]{0,1:T(8,128)(4,1)S(1)}, s32[]{:T(128)}, ...), branch_computations={%region_2.2_spmd, %region_3.5_spmd} | conditional | flops 1890062336 | bytes 27656318 | solution.py:147
  70.6 1.1 constant_dynamic-slice_fusion
  73.7 4.4 %fusion.18 = f32[4,512,128]{2,1,0:T(8,128)S(1)} fusion(bf16[512,4,128]{0,2,1:T(8,128)(2,1)S(1)} %bitcast.119, f32[4,512,512]{2,1,0:T(8,128)S(1)} %get-tuple-element.1214, f32[4,512]{1,0:T(4,128)S(1)} %max.5, pred[512,512]{0,1:T(8,128)(4,1)S(1)} %get-tuple-element.924, f32[4,512,128]{2,1,0:T(8,128)S(1)} %copy-done.1, f32[4,512]{1,0:T(4,128)S(1)} %get-tuple-element.1206), kind=kOutput, calls=%fused_computation.15 | convolution fusion | flops 1614282752 | bytes 7094272 | tf_op jit(solution)/shard_map/while/body/eval_jaxpr/cond/branch_1_fun/gqk,kge->gqe/dot_general | solution.py:142
  81.4 8.6 %conditional.8 = ((f32[4,512]{1,0:T(4,128)S(1)}, f32[4,512]{1,0:T(4,128)S(1)}, f32[4,512,128]{2,1,0:T(8,128)})) conditional(s32[]{:T(128)} %convert_element_type.120, (f32[4,512]{1,0:T(4,128)S(1)}, f32[4,512]{1,0:T(4,128)S(1)}, f32[4,512,128]{2,1,0:T(8,128)}) %tuple.160, (pred[512,512]{0,1:T(8,128)(4,1)S(1)}, s32[]{:T(128)}, ...), branch_computations={%region_2.2_spmd, %region_3.5_spmd} | conditional | flops 1890062336 | bytes 27656318 | solution.py:147
  81.4 1.1 constant_dynamic-slice_fusion
  84.5 4.4 %fusion.18 = f32[4,512,128]{2,1,0:T(8,128)S(1)} fusion(bf16[512,4,128]{0,2,1:T(8,128)(2,1)S(1)} %bitcast.119, f32[4,512,512]{2,1,0:T(8,128)S(1)} %get-tuple-element.1214, f32[4,512]{1,0:T(4,128)S(1)} %max.5, pred[512,512]{0,1:T(8,128)(4,1)S(1)} %get-tuple-element.924, f32[4,512,128]{2,1,0:T(8,128)S(1)} %copy-done.1, f32[4,512]{1,0:T(4,128)S(1)} %get-tuple-element.1206), kind=kOutput, calls=%fused_computation.15 | convolution fusion | flops 1614282752 | bytes 7094272 | tf_op jit(solution)/shard_map/while/body/eval_jaxpr/cond/branch_1_fun/gqk,kge->gqe/dot_general | solution.py:142
  92.2 8.6 %conditional.8 = ((f32[4,512]{1,0:T(4,128)S(1)}, f32[4,512]{1,0:T(4,128)S(1)}, f32[4,512,128]{2,1,0:T(8,128)})) conditional(s32[]{:T(128)} %convert_element_type.120, (f32[4,512]{1,0:T(4,128)S(1)}, f32[4,512]{1,0:T(4,128)S(1)}, f32[4,512,128]{2,1,0:T(8,128)}) %tuple.160, (pred[512,512]{0,1:T(8,128)(4,1)S(1)}, s32[]{:T(128)}, ...), branch_computations={%region_2.2_spmd, %region_3.5_spmd} | conditional | flops 1890062336 | bytes 27656318 | solution.py:147
  92.2 1.1 constant_dynamic-slice_fusion
  95.3 4.4 %fusion.18 = f32[4,512,128]{2,1,0:T(8,128)S(1)} fusion(bf16[512,4,128]{0,2,1:T(8,128)(2,1)S(1)} %bitcast.119, f32[4,512,512]{2,1,0:T(8,128)S(1)} %get-tuple-element.1214, f32[4,512]{1,0:T(4,128)S(1)} %max.5, pred[512,512]{0,1:T(8,128)(4,1)S(1)} %get-tuple-element.924, f32[4,512,128]{2,1,0:T(8,128)S(1)} %copy-done.1, f32[4,512]{1,0:T(4,128)S(1)} %get-tuple-element.1206), kind=kOutput, calls=%fused_computation.15 | convolution fusion | flops 1614282752 | bytes 7094272 | tf_op jit(solution)/shard_map/while/body/eval_jaxpr/cond/branch_1_fun/gqk,kge->gqe/dot_general | solution.py:142
  102.9 8.6 %conditional.8 = ((f32[4,512]{1,0:T(4,128)S(1)}, f32[4,512]{1,0:T(4,128)S(1)}, f32[4,512,128]{2,1,0:T(8,128)})) conditional(s32[]{:T(128)} %convert_element_type.120, (f32[4,512]{1,0:T(4,128)S(1)}, f32[4,512]{1,0:T(4,128)S(1)}, f32[4,512,128]{2,1,0:T(8,128)}) %tuple.160, (pred[512,512]{0,1:T(8,128)(4,1)S(1)}, s32[]{:T(128)}, ...), branch_computations={%region_2.2_spmd, %region_3.5_spmd} | conditional | flops 1890062336 | bytes 27656318 | solution.py:147
  103.0 1.1 constant_dynamic-slice_fusion
  106.1 4.4 %fusion.18 = f32[4,512,128]{2,1,0:T(8,128)S(1)} fusion(bf16[512,4,128]{0,2,1:T(8,128)(2,1)S(1)} %bitcast.119, f32[4,512,512]{2,1,0:T(8,128)S(1)} %get-tuple-element.1214, f32[4,512]{1,0:T(4,128)S(1)} %max.5, pred[512,512]{0,1:T(8,128)(4,1)S(1)} %get-tuple-element.924, f32[4,512,128]{2,1,0:T(8,128)S(1)} %copy-done.1, f32[4,512]{1,0:T(4,128)S(1)} %get-tuple-element.1206), kind=kOutput, calls=%fused_computation.15 | convolution fusion | flops 1614282752 | bytes 7094272 | tf_op jit(solution)/shard_map/while/body/eval_jaxpr/cond/branch_1_fun/gqk,kge->gqe/dot_general | solution.py:142
  111.5 3.3 copy.87
  114.8 1.6 multiply_reduce_fusion
  116.5 2.5 broadcast.1269
  119.0 2.5 broadcast.1269.clone
  121.5 52.9 %while.45 = (s32[]{:T(128)}, f32[4,512,128]{2,1,0:T(8,128)S(1)}, f32[2048,512]{0,1:T(8,128)}, f32[2048,512]{0,1:T(8,128)}, s32[]{:T(128)}, /*index=5*/s32[]{:T(1...) while((s32[]{:T(128)}, f32[4,512,128]{2,1,0:T(8,128)S(1)}, ...), condition=%wide.region_12.13_spmd.clone.clone, body=%wide.region_8.12_spmd.clone.clone.sunk | while | flops 1355855872 | bytes 35949944 | solution.py:84
  123.7 11.0 %conditional.9 = ((f32[4,512,128]{2,1,0:T(8,128)S(1)}, f32[2048,512]{0,1:T(8,128)}, f32[2048,512]{0,1:T(8,128)})) conditional(s32[]{:T(128)} %convert_element_type.121, (f32[4,512,128]{2,1,0:T(8,128)S(1)}, f32[2048,512]{0,1:T(8,128)}, f32[2048,512]{0,1:T(8,128)}) %tuple.165, (pred[512,512]{0,1:T(8,128)(4,1)S(1)}, s32[]{:T(128)}, ...), branch_computations={%region_10.10_spmd, %region_11.11_spmd} | conditional | flops 1354498048 | bytes 35676240 | solution.py:202
  123.8 1.1 constant_dynamic-slice_fusion.3
  125.6 1.1 constant_dynamic-slice_fusion.2
  126.7 1.7 fusion.23
  128.3 1.2 convolution_add_fusion
  130.4 1.0 fusion.25
  131.4 3.3 constant_dynamic-update-slice_fusion
  137.0 11.0 %conditional.9 = ((f32[4,512,128]{2,1,0:T(8,128)S(1)}, f32[2048,512]{0,1:T(8,128)}, f32[2048,512]{0,1:T(8,128)})) conditional(s32[]{:T(128)} %convert_element_type.121, (f32[4,512,128]{2,1,0:T(8,128)S(1)}, f32[2048,512]{0,1:T(8,128)}, f32[2048,512]{0,1:T(8,128)}) %tuple.165, (pred[512,512]{0,1:T(8,128)(4,1)S(1)}, s32[]{:T(128)}, ...), branch_computations={%region_10.10_spmd, %region_11.11_spmd} | conditional | flops 1354498048 | bytes 35676240 | solution.py:202
  137.0 1.1 constant_dynamic-slice_fusion.3
  138.8 1.1 constant_dynamic-slice_fusion.2
  139.9 1.7 fusion.23
  141.6 1.2 convolution_add_fusion
  144.6 3.3 constant_dynamic-update-slice_fusion
  150.2 10.9 %conditional.9 = ((f32[4,512,128]{2,1,0:T(8,128)S(1)}, f32[2048,512]{0,1:T(8,128)}, f32[2048,512]{0,1:T(8,128)})) conditional(s32[]{:T(128)} %convert_element_type.121, (f32[4,512,128]{2,1,0:T(8,128)S(1)}, f32[2048,512]{0,1:T(8,128)}, f32[2048,512]{0,1:T(8,128)}) %tuple.165, (pred[512,512]{0,1:T(8,128)(4,1)S(1)}, s32[]{:T(128)}, ...), branch_computations={%region_10.10_spmd, %region_11.11_spmd} | conditional | flops 1354498048 | bytes 35676240 | solution.py:202
  150.2 1.1 constant_dynamic-slice_fusion.3
  152.1 1.1 constant_dynamic-slice_fusion.2
  153.1 1.7 fusion.23
  154.8 1.2 convolution_add_fusion
  157.9 3.2 constant_dynamic-update-slice_fusion
  163.4 11.0 %conditional.9 = ((f32[4,512,128]{2,1,0:T(8,128)S(1)}, f32[2048,512]{0,1:T(8,128)}, f32[2048,512]{0,1:T(8,128)})) conditional(s32[]{:T(128)} %convert_element_type.121, (f32[4,512,128]{2,1,0:T(8,128)S(1)}, f32[2048,512]{0,1:T(8,128)}, f32[2048,512]{0,1:T(8,128)}) %tuple.165, (pred[512,512]{0,1:T(8,128)(4,1)S(1)}, s32[]{:T(128)}, ...), branch_computations={%region_10.10_spmd, %region_11.11_spmd} | conditional | flops 1354498048 | bytes 35676240 | solution.py:202
  163.4 1.1 constant_dynamic-slice_fusion.3
  165.2 1.1 constant_dynamic-slice_fusion.2
  166.3 1.7 fusion.23
  168.0 1.2 convolution_add_fusion
  171.1 3.3 constant_dynamic-update-slice_fusion
  174.3 4.6 %copy.90 = bf16[2048,512]{1,0:T(8,128)(2,1)} copy(f32[2048,512]{0,1:T(8,128)} %get-tuple-element.990) | data formatting | bytes 6291456 | tf_op jit(solution)/shard_map/while | solution.py:84
  178.9 4.6 %copy.89 = bf16[2048,512]{1,0:T(8,128)(2,1)} copy(f32[2048,512]{0,1:T(8,128)} %get-tuple-element.989) | data formatting | bytes 6291456 | tf_op jit(solution)/shard_map/while | solution.py:84
  183.6 4.7 %pad_maximum_fusion = bf16[2048,1024]{1,0:T(8,128)(2,1)} fusion(bf16[2048,512]{1,0:T(8,128)(2,1)} %copy.90, bf16[2048,512]{1,0:T(8,128)(2,1)} %copy.89), kind=kLoop, calls=%fused_computation.90 | loop fusion | flops 8388608 | bytes 8388608 | tf_op jit(solution)/shard_map/concatenate | solution.py:30
  188.3 1.6 copy.91
  189.9 1.6 copy.92
  191.6 3.7 %all-to-all-start.1 = ((bf16[128,16,256]{0,1,2:T(8,128)(2,1)}), bf16[128,16,256]{0,1,2:T(8,128)(2,1)S(1)}, u32[]{:S(2)}, u32[]{:S(2)}) async-start(bf16[128,16,256]{0,1,2:T(8,128)(2,1)} %copy.92), calls=%async_computation.2 | async-start | bytes 2097152 | tf_op jit(solution)/shard_map/all_to_all | solution.py:251
  195.8 68.6 %reduce-scatter.2.cloned.1.call-done = bf16[128,1024]{1,0:T(8,128)(2,1)} async-done(((bf16[2048,1024]{1,0:T(8,128)(2,1)}), bf16[128,1024]{1,0:T(8,128)(2,1)}) %reduce-scatter.2.cloned.1.call-update) | async-done | bytes 262160 | tf_op jit(solution)/shard_map/reduce_scatter | solution.py:31
  264.3 1.7 slice_convert_fusion
  267.6 2.5 stack.2
  270.1 7.2 %all-to-all-start = ((bf16[16,128,1024]{2,1,0:T(8,128)(2,1)}), bf16[16,128,1024]{2,1,0:T(8,128)(2,1)}, u32[]{:S(2)}, u32[]{:S(2)}) async-start(bf16[16,128,1024]{2,1,0:T(8,128)(2,1)} %stack.2), calls=%async_computation.1 | async-start | bytes 8388608 | tf_op jit(solution)/shard_map/all_to_all | solution.py:11
  277.4 1.3 copy.93
  278.7 48.3 %all-to-all-done = bf16[16,128,1024]{2,1,0:T(8,128)(2,1)} async-done(((bf16[16,128,1024]{2,1,0:T(8,128)(2,1)}), bf16[16,128,1024]{2,1,0:T(8,128)(2,1)}, u32[]{:S(2)}, u32[]{:S(2)}) %all-to-all-start) | async-done | bytes 4194336 | tf_op jit(solution)/shard_map/all_to_all | solution.py:11
  327.0 4.5 %fusion.55 = bf16[16,1,16,1024]{3,2,1,0:T(8,128)(2,1)} fusion(bf16[16,128,16,16]{1,3,0,2:T(8,128)(2,1)} %bitcast.128, bf16[16,128,1024]{2,1,0:T(8,128)(2,1)} %all-to-all-done), kind=kOutput, calls=%fused_computation.95 | convolution fusion | flops 1074003968 | bytes 5767168 | tf_op jit(solution)/shard_map/tif,tc->ifc/dot_general | solution.py:252
  331.5 7.8 %all-to-all-start.2 = ((bf16[16,1,16,1024]{3,2,1,0:T(8,128)(2,1)}), bf16[16,1,16,1024]{3,2,1,0:T(8,128)(2,1)S(1)}, u32[]{:S(2)}, u32[]{:S(2)}) async-start(bf16[16,1,16,1024]{3,2,1,0:T(8,128)(2,1)} %fusion.55), calls=%async_computation.3 | async-start | bytes 1048576 | tf_op jit(solution)/shard_map/all_to_all | solution.py:42
  339.9 1.2 convert_element_type.92
  341.1 11.8 %all-to-all-done.2 = bf16[16,1,16,1024]{3,2,1,0:T(8,128)(2,1)S(1)} async-done(((bf16[16,1,16,1024]{3,2,1,0:T(8,128)(2,1)}), bf16[16,1,16,1024]{3,2,1,0:T(8,128)(2,1)S(1)}, u32[]{:S(2)}, u32[]{:S(2)}) %all-to-all-start.2) | async-done | bytes 524320 | tf_op jit(solution)/shard_map/all_to_all | solution.py:42
  (119 shorter events, 43.1 us)
Async XLA Ops:
  7.2 5.5 %copy-start.4 = (bf16[1,128,2048]{2,1,0:T(8,128)(2,1)S(1)}, bf16[1,128,2048]{2,1,0:T(8,128)(2,1)}, u32[]{:S(2)}) copy-start(bf16[1,128,2048]{2,1,0:T(8,128)(2,1)} %param.17) | copy-start | bytes 1572868
  7.2 56.1 %all-gather.2.cloned.1.call-start = ((), (), s32[]{:S(2)}) async-start(), calls=%async_computation.4 | async-start | bytes 4456448 | tf_op jit(solution)/shard_map/all_gather | solution.py:24
  8.3 6.3 %copy-start.5 = (s32[1,3]{1,0:T(1,128)S(1)}, s32[1,3]{1,0:T(1,128)}, u32[]{:S(2)}) copy-start(s32[1,3]{1,0:T(1,128)} %param.19) | copy-start | bytes 40
  10.1 254.2 %reduce-scatter.2.cloned.1.call-start = ((), (), s32[]{:S(2)}) async-start(), calls=%async_computation.5 | async-start | bytes 4456448 | tf_op jit(solution)/shard_map/reduce_scatter | solution.py:31
  71.8 2.0 copy-start.1
  78.2 1.0 copy-start.2
  82.5 2.0 copy-start.1
  89.0 1.0 copy-start.2
  93.3 2.0 copy-start.1
  99.7 1.0 copy-start.2
  104.1 2.0 copy-start.1
  110.5 1.0 copy-start.2
  111.5 3.3 copy-start
  116.5 5.0 %copy-start.3 = (bf16[4,512,128]{1,2,0:T(8,128)(2,1)S(1)}, bf16[4,512,128]{1,2,0:T(8,128)(2,1)}, u32[]{:S(2)}) copy-start(bf16[4,512,128]{1,2,0:T(8,128)(2,1)} %reshape.347) | copy-start | bytes 1572868
  191.6 76.0 %all-to-all-start.1 = ((bf16[128,16,256]{0,1,2:T(8,128)(2,1)}), bf16[128,16,256]{0,1,2:T(8,128)(2,1)S(1)}, u32[]{:S(2)}, u32[]{:S(2)}) async-start(bf16[128,16,256]{0,1,2:T(8,128)(2,1)} %copy.92), calls=%async_computation.2 | async-start | bytes 2097152 | tf_op jit(solution)/shard_map/all_to_all | solution.py:251
  270.1 56.9 %all-to-all-start = ((bf16[16,128,1024]{2,1,0:T(8,128)(2,1)}), bf16[16,128,1024]{2,1,0:T(8,128)(2,1)}, u32[]{:S(2)}, u32[]{:S(2)}) async-start(bf16[16,128,1024]{2,1,0:T(8,128)(2,1)} %stack.2), calls=%async_computation.1 | async-start | bytes 8388608 | tf_op jit(solution)/shard_map/all_to_all | solution.py:11
  331.5 21.4 %all-to-all-start.2 = ((bf16[16,1,16,1024]{3,2,1,0:T(8,128)(2,1)}), bf16[16,1,16,1024]{3,2,1,0:T(8,128)(2,1)S(1)}, u32[]{:S(2)}, u32[]{:S(2)}) async-start(bf16[16,1,16,1024]{3,2,1,0:T(8,128)(2,1)} %fusion.55), calls=%async_computation.3 | async-start | bytes 1048576 | tf_op jit(solution)/shard_map/all_to_all | solution.py:42
Sparse Core Ops, SparseCore 0:
  10.2 53.0 all-gather.1
  188.4 75.8 reduce-scatter.1
